TPU v7x, 256 devices: a whole 4x4x8 slice. The times are simulated.
256 devices in a mesh: gx: 8 (over z), gy: 2 (over core), gz: 16 (over y, x).
Axes of the slice: x: 4, y: 4, z: 8, core: 2. Of those that a mesh axis runs over, the one named last changes fastest.
Arguments:
- pair: bfloat16 [128, 1024, 1024], P('gz', 'gx', 'gy'), may hold values from -6 to 6
- pair_mask: int32 [1024, 1024], P('gx', 'gy'), may hold values from 0 to 1, as said below
- input_gain: float32 [128], replicated, may hold values from 0.1 to 1.9
- input_weights: bfloat16 [4, 128, 128], replicated, may hold values from -0.5 to 0.5
- out_gate_weight: bfloat16 [128, 128], replicated, may hold values from -0.5 to 0.5
- hidden_gain: float32 [128], replicated, may hold values from 0.1 to 1.9
- out_weight: bfloat16 [128, 128], replicated, may hold values from -0.5 to 0.5
Outputs:
- update: bfloat16 [128, 1024, 1024], P('gz', 'gx', 'gy')
Inputs may be any that keep to these rules, and one draw needn't show every extreme that they name: pair_mask[r, s] = m[r] * m[s] for a 0/1 residue mask m of the draw that is 0 for all r >= L, for one crop length L with 512 < L <= 1024; residues below L may also be 0.
All inputs are finite; a program needn't handle non-finite values.
Results may differ from a plain program's by a relative error of at most 0.011.
Values may be sent and summed in bfloat16 or wider, within the bound.
A program may use at most 64 MiB of HBM per device.

v0:
```python
import jax
import jax.numpy as jnp
from jax import lax
from jax.sharding import PartitionSpec as P

EPSILON = 1e-05


def side_by_side(arrays, axis, split_dim, concat_dim, along):
    widths = [a.shape[along] for a in arrays]
    both = jnp.concatenate(arrays, axis=along)
    whole = lax.all_to_all(both, axis, split_axis=split_dim, concat_axis=concat_dim, tiled=True)
    return tuple(jnp.split(whole, [sum(widths[:k]) for k in range(1, len(widths))], axis=along))


def from_everyone(value, axis):
    copies = jnp.broadcast_to(value, (lax.axis_size(axis), *value.shape))
    return lax.all_to_all(copies, axis, split_axis=0, concat_axis=0, tiled=True)


def joined_along(pieces, dim):
    dims = list(pieces.shape[1:])
    dims[dim] *= pieces.shape[0]
    return jnp.moveaxis(pieces, 0, dim).reshape(dims)


def gather_directly(value, axis, dim):
    pieces = from_everyone(value, axis)
    return joined_along(pieces, dim)


def gated_sides(weights, normed, mask_values, hidden):
    joined = jnp.concatenate([weights[0], weights[1]], axis=1)
    product = jnp.einsum("dk,drs->krs", joined, normed, preferred_element_type=jnp.float32)
    return (mask_values * jax.nn.sigmoid(product[:hidden]) * product[hidden:]).astype(jnp.bfloat16)


def shards(pair, pair_mask, input_gain, input_weights, out_gate_weight, hidden_gain, out_weight):
    all_hidden = hidden_gain.shape[0]
    mask_values = pair_mask.astype(jnp.float32)
    share_width = pair.shape[2] // lax.axis_size("gz")
    shared_pairs = lax.all_to_all(pair, "gz", split_axis=2, concat_axis=0, tiled=True)
    share_mask = lax.dynamic_slice_in_dim(
        mask_values, lax.axis_index("gz") * share_width, share_width, 1
    )
    values = shared_pairs.astype(jnp.float32)
    average = jnp.mean(values, axis=0)
    spread = jnp.mean(jnp.square(values - average), axis=0)
    normed = ((values - average) * lax.rsqrt(spread + EPSILON) * input_gain[:, None, None]).astype(
        jnp.bfloat16
    )
    left_share = gated_sides(input_weights[0:2], normed, share_mask, all_hidden)
    right_share = gated_sides(input_weights[2:4], normed, share_mask, all_hidden)
    gate_share = jax.nn.sigmoid(
        jnp.einsum("dc,drs->crs", out_gate_weight, normed, preferred_element_type=jnp.float32)
    )
    left_side, right_side = side_by_side((left_share, right_share), "gz", 0, 2, 1)
    gate = lax.all_to_all(
        gate_share.astype(jnp.bfloat16), "gz", split_axis=0, concat_axis=2, tiled=True
    ).astype(gate_share.dtype)
    left_panels = gather_directly(left_side, "gy", 2)
    row_blocks = lax.all_to_all(left_panels, "gx", split_axis=2, concat_axis=1, tiled=True)
    triangle = jnp.einsum(
        "cki,ckj->icj",
        row_blocks,
        lax.all_gather(right_side, "gx", axis=1, tiled=True),
        preferred_element_type=jnp.float32,
    )
    triangle_part = lax.all_to_all(
        triangle.astype(jnp.bfloat16), "gz", split_axis=2, concat_axis=1, tiled=True
    ).astype(triangle.dtype)
    hidden_mean = jnp.mean(triangle_part, axis=1)
    hidden_spread = jnp.mean(jnp.square(triangle_part - hidden_mean[:, None, :]), axis=1)
    part_normed = (
        (triangle_part - hidden_mean[:, None, :])
        * lax.rsqrt(hidden_spread + EPSILON)[:, None, :]
        * hidden_gain[None, :, None]
    ).astype(jnp.bfloat16)
    projected_part = jnp.einsum(
        "hc,ihj->cij", out_weight, part_normed, preferred_element_type=jnp.float32
    )
    projected = lax.all_to_all(
        projected_part.astype(jnp.bfloat16), "gz", split_axis=0, concat_axis=2, tiled=True
    ).astype(projected_part.dtype)
    return (mask_values * gate * projected).astype(jnp.bfloat16)


def solution(mesh):
    placed = (P("gz", "gx", "gy"), P("gx", "gy"), P(), P(), P(), P(), P())
    return jax.shard_map(
        shards, mesh=mesh, in_specs=placed, out_specs=P("gz", "gx", "gy"), check_vma=False
    )
```

profile of v0, /device:TPU:8, one launch (start us, length us, event | category | flops | bytes accessed | tf_op | source)
XLA Modules:
  0.0 287.8 jit_solution(9119791772001024543)
XLA Ops:
  6.5 2.5 copy.55
  9.0 7.4 %all-to-all-start = ((bf16[8,128,512]{1,0,2:T(8,128)(2,1)}), bf16[8,128,512]{1,0,2:T(8,128)(2,1)S(1)}, u32[]{:S(2)}, u32[]{:S(2)}) async-start(bf16[8,128,512]{1,0,2:T(8,128)(2,1)} %copy.55), calls=%async_computation | async-start | bytes 2097152 | tf_op jit(solution)/shard_map/all_to_all | solution.py:42
  16.7 14.3 %all-to-all-done = bf16[8,128,512]{1,0,2:T(8,128)(2,1)S(1)} async-done(((bf16[8,128,512]{1,0,2:T(8,128)(2,1)}), bf16[8,128,512]{1,0,2:T(8,128)(2,1)S(1)}, u32[]{:S(2)}, u32[]{:S(2)}) %all-to-all-start) | async-done | bytes 1048608 | tf_op jit(solution)/shard_map/all_to_all | solution.py:42
  32.1 0.4 copy-done.5
  32.8 1.0 copy.58
  33.8 0.7 fusion.26
  34.5 0.7 fusion.23
  35.2 1.3 fusion.5
  36.6 3.0 %copy.64 = bf16[128,256,32]{1,2,0:T(8,128)(2,1)} copy(bf16[128,256,32]{0,1,2:T(8,128)(2,1)S(1)} %pad_maximum_fusion) | data formatting | bytes 4194304 | tf_op jit(solution)/shard_map/concatenate | solution.py:11
  39.6 31.9 %all_to_all.77 = bf16[128,256,32]{1,2,0:T(8,128)(2,1)S(1)} all-to-all(bf16[128,256,32]{1,2,0:T(8,128)(2,1)} %copy.64), channel_id=1, replica_groups=mesh['gx'=8,'gy'=2,'gz'=16] {'gz'}, dimensions={0} | all-to-all | bytes 4194304 | tf_op jit(solution)/shard_map/all_to_all | solution.py:12
  71.7 1.5 fusion.33
  73.7 5.4 %all_to_all.78 = bf16[2,8,128,512]{2,3,1,0:T(8,128)(2,1)S(1)} all-to-all(bf16[2,8,128,512]{2,3,1,0:T(8,128)(2,1)S(1)} %broadcast_in_dim.2), channel_id=1, replica_groups=mesh['gx'=8,'gy'=2,'gz'=16] {'gy'}, dimensions={0} | all-to-all | bytes 4194304 | tf_op jit(solution)/shard_map/all_to_all | solution.py:18
  79.3 1.4 copy.67
  80.6 78.6 %all_to_all.79 = bf16[8,128,1024]{1,0,2:T(8,128)(2,1)S(1)} all-to-all(bf16[8,128,1024]{1,0,2:T(8,128)(2,1)S(1)} %copy.67), channel_id=1, replica_groups=mesh['gx'=8,'gy'=2,'gz'=16] {'gx'}, dimensions={2} | all-to-all | bytes 4194304 | tf_op jit(solution)/shard_map/all_to_all | solution.py:62
  159.2 2.9 copy.69
  162.1 54.3 %all-gather.2.cloned.1.call-done = bf16[8,1024,512]{1,2,0:T(8,128)(2,1)} async-done(((bf16[8,128,512]{1,2,0:T(8,128)(2,1)}), bf16[8,1024,512]{1,2,0:T(8,128)(2,1)}) %all-gather.2.cloned.1.call-update) | async-done | bytes 8388624 | tf_op jit(solution)/shard_map/all_gather | solution.py:66
  216.4 6.3 %fusion.17 = bf16[128,8,512]{0,2,1:T(8,128)(2,1)S(1)} fusion(bf16[8,1024,512]{1,2,0:T(8,128)(2,1)} %all-gather.2.cloned.1.call-done, bf16[8,1024,128]{2,1,0:T(8,128)(2,1)} %bitcast.102), kind=kOutput, calls=%fused_computation.35 | convolution fusion | flops 1074266112 | bytes 11534336 | tf_op jit(solution)/shard_map/cki,ckj->icj/dot_general | solution.py:63
  222.7 1.7 copy.70
  224.3 8.4 %all-to-all-start.5 = ((bf16[128,8,512]{0,1,2:T(8,128)(2,1)}), bf16[128,8,512]{0,1,2:T(8,128)(2,1)S(1)}, u32[]{:S(2)}, u32[]{:S(2)}) async-start(bf16[128,8,512]{0,1,2:T(8,128)(2,1)} %copy.70), calls=%async_computation.5 | async-start | bytes 2097152 | tf_op jit(solution)/shard_map/all_to_all | solution.py:69
  232.8 0.7 fusion.19
  233.5 1.7 copy.59
  235.2 9.0 %all-to-all-done.5 = bf16[128,8,512]{0,1,2:T(8,128)(2,1)S(1)} async-done(((bf16[128,8,512]{0,1,2:T(8,128)(2,1)}), bf16[128,8,512]{0,1,2:T(8,128)(2,1)S(1)}, u32[]{:S(2)}, u32[]{:S(2)}) %all-to-all-start.5) | async-done | bytes 1048608 | tf_op jit(solution)/shard_map/all_to_all | solution.py:69
  244.1 6.0 %all-to-all-start.1 = ((bf16[128,128,32]{1,2,0:T(8,128)(2,1)}), bf16[128,128,32]{1,2,0:T(8,128)(2,1)S(1)}, u32[]{:S(2)}, u32[]{:S(2)}) async-start(bf16[128,128,32]{1,2,0:T(8,128)(2,1)} %copy.59), calls=%async_computation.1 | async-start | bytes 2097152 | tf_op jit(solution)/shard_map/all_to_all | solution.py:58
  251.7 0.6 fusion.18
  252.3 1.7 copy.74
  253.9 6.9 %all-to-all-done.1 = bf16[128,128,32]{1,2,0:T(8,128)(2,1)S(1)} async-done(((bf16[128,128,32]{1,2,0:T(8,128)(2,1)}), bf16[128,128,32]{1,2,0:T(8,128)(2,1)S(1)}, u32[]{:S(2)}, u32[]{:S(2)}) %all-to-all-start.1) | async-done | bytes 1048608 | tf_op jit(solution)/shard_map/all_to_all | solution.py:58
  260.9 6.3 %all-to-all-start.6 = ((bf16[128,128,32]{1,2,0:T(8,128)(2,1)}), bf16[128,128,32]{1,2,0:T(8,128)(2,1)S(1)}, u32[]{:S(2)}, u32[]{:S(2)}) async-start(bf16[128,128,32]{1,2,0:T(8,128)(2,1)} %copy.74), calls=%async_computation.6 | async-start | bytes 2097152 | tf_op jit(solution)/shard_map/all_to_all | solution.py:82
  267.1 0.8 copy.54
  268.5 9.5 %all-to-all-done.6 = bf16[128,128,32]{1,2,0:T(8,128)(2,1)S(1)} async-done(((bf16[128,128,32]{1,2,0:T(8,128)(2,1)}), bf16[128,128,32]{1,2,0:T(8,128)(2,1)S(1)}, u32[]{:S(2)}, u32[]{:S(2)}) %all-to-all-start.6) | async-done | bytes 1048608 | tf_op jit(solution)/shard_map/all_to_all | solution.py:82
  278.4 0.8 copy-done.1
  279.2 0.4 fusion.10
  279.6 1.3 copy.76
  (40 shorter events, 5.1 us)
Async XLA Ops:
  6.5 226.2 %copy-start = (bf16[128,128]{1,0:T(8,128)(2,1)S(1)}, bf16[128,128]{1,0:T(8,128)(2,1)}, u32[]{:S(2)}) copy-start(bf16[128,128]{1,0:T(8,128)(2,1)} %param.11) | copy-start | bytes 98308
  6.5 9.9 %copy-start.2 = (s32[128,512]{1,0:T(8,128)S(1)}, s32[128,512]{1,0:T(8,128)}, u32[]{:S(2)}) copy-start(s32[128,512]{1,0:T(8,128)} %param.8) | copy-start | bytes 786436
  6.5 10.1 %copy-start.3 = (bf16[4,128,128]{2,1,0:T(8,128)(2,1)S(1)}, bf16[4,128,128]{2,1,0:T(8,128)(2,1)}, u32[]{:S(2)}) copy-start(bf16[4,128,128]{2,1,0:T(8,128)(2,1)} %param.10) | copy-start | bytes 393220
  9.0 22.0 %all-to-all-start = ((bf16[8,128,512]{1,0,2:T(8,128)(2,1)}), bf16[8,128,512]{1,0,2:T(8,128)(2,1)S(1)}, u32[]{:S(2)}, u32[]{:S(2)}) async-start(bf16[8,128,512]{1,0,2:T(8,128)(2,1)} %copy.55), calls=%async_computation | async-start | bytes 2097152 | tf_op jit(solution)/shard_map/all_to_all | solution.py:42
  16.4 200.0 %all-gather.2.cloned.1.call-start = ((), (), s32[]{:S(2)}) async-start(), calls=%async_computation.7 | async-start | bytes 9437184 | tf_op jit(solution)/shard_map/all_gather | solution.py:66
  31.9 0.7 copy-start.5
  224.3 19.8 %all-to-all-start.5 = ((bf16[128,8,512]{0,1,2:T(8,128)(2,1)}), bf16[128,8,512]{0,1,2:T(8,128)(2,1)S(1)}, u32[]{:S(2)}, u32[]{:S(2)}) async-start(bf16[128,8,512]{0,1,2:T(8,128)(2,1)} %copy.70), calls=%async_computation.5 | async-start | bytes 2097152 | tf_op jit(solution)/shard_map/all_to_all | solution.py:69
  244.1 16.7 %all-to-all-start.1 = ((bf16[128,128,32]{1,2,0:T(8,128)(2,1)}), bf16[128,128,32]{1,2,0:T(8,128)(2,1)S(1)}, u32[]{:S(2)}, u32[]{:S(2)}) async-start(bf16[128,128,32]{1,2,0:T(8,128)(2,1)} %copy.59), calls=%async_computation.1 | async-start | bytes 2097152 | tf_op jit(solution)/shard_map/all_to_all | solution.py:58
  250.7 0.7 copy-start.6
  250.9 0.8 copy-start.4
  260.9 17.1 %all-to-all-start.6 = ((bf16[128,128,32]{1,2,0:T(8,128)(2,1)}), bf16[128,128,32]{1,2,0:T(8,128)(2,1)S(1)}, u32[]{:S(2)}, u32[]{:S(2)}) async-start(bf16[128,128,32]{1,2,0:T(8,128)(2,1)} %copy.74), calls=%async_computation.6 | async-start | bytes 2097152 | tf_op jit(solution)/shard_map/all_to_all | solution.py:82
  278.3 1.0 copy-start.1
Sparse Core Ops, SparseCore 0:
  73.4 142.9 all-gather.1
where the time goes:
time: 293 us; the launch traced here: 288 us
  blocking collectives  116 us (40%)
  waiting for transfers between devices  94 us (32%)
  starting transfers between devices  28.1 us (10%)
  local copies, waits for them, and re-layouts  22.5 us (8%)
  between operations  13.6 us (5%)
  matrix products  8.93 us (3%)
  other arithmetic  4.72 us (2%)
    all_to_all x1, blocking collectives, shards(): lax.all_to_all(left_panels, 'gx', split_axis=2, concat_axis=1, tiled=True)  78.6 us
    all_gather x1, waiting for transfers between devices, shards(): lax.all_gather(right_side, 'gx', axis=1, tiled=True)  54.3 us
    all_to_all x1, blocking collectives, side_by_side(): lax.all_to_all(both, axis, split_axis=split_dim, concat_axis=concat_dim,...  31.9 us
    all_to_all x1, waiting for transfers between devices, shards(): lax.all_to_all(pair, 'gz', split_axis=2, concat_axis=0, tiled=True)  14.3 us
    all_to_all x1, waiting for transfers between devices, shards(): lax.all_to_all(projected_part.astype(jnp.bfloat16), 'gz', split_axis=0, c...  9.51 us
    all_to_all x1, waiting for transfers between devices, shards(): lax.all_to_all(triangle.astype(jnp.bfloat16), 'gz', split_axis=2, concat_...  8.96 us
    all_to_all x1, starting transfers between devices, shards(): lax.all_to_all(triangle.astype(jnp.bfloat16), 'gz', split_axis=2, concat_...  8.43 us
    all_to_all x1, starting transfers between devices, shards(): lax.all_to_all(pair, 'gz', split_axis=2, concat_axis=0, tiled=True)  7.39 us
  transfers between devices with their start and end apart: 5, of which 5 were waited for; matrix products, arithmetic and copies ran while one was open for 4% of the time, Pallas kernels for 0%

commit v1 on v0

v1 whole, which is shorter than its diff:
```python
import jax
import jax.numpy as jnp
from jax import lax
from jax.sharding import PartitionSpec as P

EPSILON = 1e-05


def layer_norm(values, gains):
    average = jnp.mean(values, axis=0)
    spread = jnp.mean(jnp.square(values - average), axis=0)
    normed = (values - average) * lax.rsqrt(spread + EPSILON) * gains[:, None, None]
    return normed.astype(jnp.bfloat16)


def exchange(value, axis, split_dim, concat_dim):
    return lax.all_to_all(value, axis, split_axis=split_dim, concat_axis=concat_dim, tiled=True)


def shards(pair, pair_mask, input_gain, input_weights, out_gate_weight, hidden_gain, out_weight):
    channels = input_gain.shape[0]
    hidden = hidden_gain.shape[0]
    rows = pair.shape[1] // lax.axis_size("gz")
    share_mask = lax.dynamic_slice_in_dim(
        pair_mask, lax.axis_index("gz") * rows, rows, 0
    ).astype(jnp.float32)

    normed = layer_norm(exchange(pair, "gz", 1, 0).astype(jnp.float32), input_gain)
    weights = jnp.concatenate([*input_weights, out_gate_weight], axis=1)
    product = jnp.einsum("dk,drs->krs", weights, normed, preferred_element_type=jnp.float32)
    left_gate, left, right_gate, right = (product[k * hidden : (k + 1) * hidden] for k in range(4))
    gate = share_mask * jax.nn.sigmoid(product[4 * hidden :])
    sides = jnp.stack(
        [
            (share_mask * jax.nn.sigmoid(left_gate) * left).astype(jnp.bfloat16),
            (share_mask * jax.nn.sigmoid(right_gate) * right).astype(jnp.bfloat16),
        ],
        axis=1,
    )

    sides = exchange(sides, "gz", 0, 2)
    sides = exchange(sides, "gx", 0, 2)
    left_side = lax.all_gather(sides[:, 0], "gy", axis=2, tiled=True)
    triangle = jnp.einsum(
        "hki,hkj->hij", left_side, sides[:, 1], preferred_element_type=jnp.float32
    ).astype(jnp.bfloat16)
    triangle = exchange(triangle, "gx", 1, 0)
    triangle = exchange(triangle, "gz", 1, 0)

    hidden_normed = layer_norm(triangle.astype(jnp.float32), hidden_gain)
    projected = jnp.einsum(
        "hc,hij->cij", out_weight, hidden_normed, preferred_element_type=jnp.float32
    )
    update = (gate * projected).astype(jnp.bfloat16)
    return exchange(update, "gz", 0, 1)


def solution(mesh):
    placed = (P("gz", "gx", "gy"), P("gx", "gy"), P(), P(), P(), P(), P())
    return jax.shard_map(
        shards, mesh=mesh, in_specs=placed, out_specs=P("gz", "gx", "gy"), check_vma=False
    )
```

time: 293 us -> 247 us (0.84); the launches traced: 288 us -> 246 us
  waiting for transfers between devices: 94 us -> 23.7 us
  blocking collectives: 116 us -> 167 us
  starting transfers between devices: 28.1 us -> 7.43 us
  local copies, waits for them, and re-layouts: 22.5 us -> 15.8 us
  other arithmetic: 4.72 us -> 11.2 us
    all_to_all x3 -> x5, blocking collectives: 116 us -> 167 us  [exchange(): lax.all_to_all(value, axis, split_axis=split_dim, concat_axis=concat_dim,...]
    all_gather x1, waiting for transfers between devices: 54.3 us -> 10.6 us  [shards(): left_side = lax.all_gather(sides[:, 0], 'gy', axis=2, tiled=True)]
    all_to_all x4 -> x1, waiting for transfers between devices: 39.7 us -> 13.1 us  [exchange(): lax.all_to_all(value, axis, split_axis=split_dim, concat_axis=concat_dim,...]
    all_to_all x4 -> x1, starting transfers between devices: 28.1 us -> 7.39 us  [exchange(): lax.all_to_all(value, axis, split_axis=split_dim, concat_axis=concat_dim,...]
    unnamed x0 -> x1, other arithmetic: none -> 7.04 us
    unnamed x15 -> x26, local copies, waits for them, and re-layouts: 3.76 us -> 9.09 us
    convert_element_type x9 -> x3, local copies, waits for them, and re-layouts: 7.31 us -> 2.43 us  [the longest x1 1.62 us: shards(): triangle = jnp.einsum('hki,hkj->hij', left_side, sides[:, 1], preferred_e...]
    concatenate x1, local copies, waits for them, and re-layouts: 3 us -> 0.01 us  [shards(): weights = jnp.concatenate([*input_weights, out_gate_weight], axis=1)]
  transfers between devices with their start and end apart: 5 -> 2, of which waited for: 5 -> 2; matrix products, arithmetic and copies ran while one was open for 4% -> 1% of each run, Pallas kernels for 0% -> 0%
where the time goes in v1:
time: 247 us; the launch traced here: 246 us
  blocking collectives  167 us (68%)
  waiting for transfers between devices  23.7 us (10%)
  local copies, waits for them, and re-layouts  15.8 us (6%)
  between operations  13.7 us (6%)
  other arithmetic  11.2 us (5%)
  starting transfers between devices  7.43 us (3%)
  matrix products  7.01 us (3%)
    all_to_all x5, blocking collectives, exchange(): lax.all_to_all(value, axis, split_axis=split_dim, concat_axis=concat_dim,...  167 us
    all_to_all x1, waiting for transfers between devices, exchange(): lax.all_to_all(value, axis, split_axis=split_dim, concat_axis=concat_dim,...  13.1 us
    all_gather x1, waiting for transfers between devices, shards(): left_side = lax.all_gather(sides[:, 0], 'gy', axis=2, tiled=True)  10.6 us
    unnamed x26, local copies, waits for them, and re-layouts  9.09 us
    all_to_all x1, starting transfers between devices, exchange(): lax.all_to_all(value, axis, split_axis=split_dim, concat_axis=concat_dim,...  7.39 us
    unnamed x1, other arithmetic  7.04 us
  transfers between devices with their start and end apart: 2, of which 2 were waited for; matrix products, arithmetic and copies ran while one was open for 1% of the time, Pallas kernels for 0%

profile of v1, /device:TPU:8, one launch (start us, length us, event | category | flops | bytes accessed | tf_op | source)
XLA Modules:
  0.0 245.7 jit_solution(13325242700693101154)
XLA Ops:
  6.5 2.8 %copy.62 = bf16[8,128,512]{2,0,1:T(8,128)(2,1)} copy(bf16[8,128,512]{2,1,0:T(8,128)(2,1)} %param.7) | data formatting | bytes 2097152 | tf_op args[0]
  9.4 7.4 %all-to-all-start = ((bf16[8,128,512]{2,0,1:T(8,128)(2,1)}), bf16[8,128,512]{2,0,1:T(8,128)(2,1)S(1)}, u32[]{:S(2)}, u32[]{:S(2)}) async-start(bf16[8,128,512]{2,0,1:T(8,128)(2,1)} %copy.62), calls=%async_computation | async-start | bytes 2097152 | tf_op jit(solution)/shard_map/all_to_all | solution.py:17
  17.5 0.7 dynamic-slice_convert_fusion
  18.2 13.1 %all-to-all-done = bf16[8,128,512]{2,0,1:T(8,128)(2,1)S(1)} async-done(((bf16[8,128,512]{2,0,1:T(8,128)(2,1)}), bf16[8,128,512]{2,0,1:T(8,128)(2,1)S(1)}, u32[]{:S(2)}, u32[]{:S(2)}) %all-to-all-start) | async-done | bytes 1048608 | tf_op jit(solution)/shard_map/all_to_all | solution.py:17
  31.5 0.3 multiply_reduce_fusion.1
  31.8 1.6 fusion.30
  33.5 1.4 fusion.38
  34.8 2.6 %copy-done.1 = f32[640,8,512]{2,0,1:T(8,128)} copy-done((f32[640,8,512]{2,0,1:T(8,128)}, f32[640,8,512]{2,0,1:T(8,128)S(1)}, u32[]{:S(2)}) %copy-start.1) | copy-done | bytes 10485784
  37.6 1.2 copy.64
  38.8 31.3 %all_to_all.84 = bf16[128,2,8,512]{3,2,1,0:T(8,128)(2,1)S(1)} all-to-all(bf16[128,2,8,512]{3,2,1,0:T(8,128)(2,1)S(1)} %copy.64), channel_id=1, replica_groups=mesh['gx'=8,'gy'=2,'gz'=16] {'gz'}, dimensions={0} | all-to-all | bytes 4194304 | tf_op jit(solution)/shard_map/all_to_all | solution.py:17
  70.4 58.4 %all_to_all.85 = bf16[8,2,128,512]{3,2,1,0:T(8,128)(2,1)S(1)} all-to-all(bf16[8,2,128,512]{3,2,1,0:T(8,128)(2,1)S(1)} %bitcast.101), channel_id=1, replica_groups=mesh['gx'=8,'gy'=2,'gz'=16] {'gx'}, dimensions={0} | all-to-all | bytes 4194304 | tf_op jit(solution)/shard_map/all_to_all | solution.py:17
  129.0 1.0 slice.33
  130.0 10.6 %all-gather.3.cloned.1.call-done = bf16[1,1,1024,1024]{3,2,1,0:T(8,128)(2,1)} async-done(((bf16[1,1,1024,512]{3,2,1,0:T(8,128)(2,1)}), bf16[1,1,1024,1024]{3,2,1,0:T(8,128)(2,1)}) %all-gather.3.cloned.1.call-update) | async-done | bytes 2097168 | tf_op jit(solution)/shard_map/all_gather | solution.py:43
  140.6 2.9 %fusion.27 = bf16[1,1024,512]{2,1,0:T(8,128)(2,1)S(1)} fusion(bf16[1,1,1024,1024]{3,2,1,0:T(8,128)(2,1)} %all-gather.3.cloned.1.call-done, bf16[1,2,1024,512]{3,2,1,0:T(8,128)(2,1)S(1)} %bitcast.104), kind=kOutput, calls=%fused_computation.38 | convolution fusion | flops 1074266112 | bytes 4194304 | tf_op jit(solution)/shard_map/hki,hkj->hij/dot_general | solution.py:44
  143.5 1.6 copy.93
  145.1 0.5 broadcast.58
  145.6 7.0 %reduce.4 = bf16[1024,512]{1,0:T(8,128)(2,1)S(1)} reduce(bf16[1024,1,512]{2,1,0:T(2,128)(2,1)S(1)} %bitcast.99, bf16[]{:T(256)} %broadcast.58), dimensions={1}, to_apply=%bitcast.95.reduce_sub_computation | reduce | bytes 2097154
  152.7 0.8 reshape.55
  153.5 36.0 %all_to_all.86 = bf16[8,2,32768]{2,1,0:T(2,128)(2,1)S(1)} all-to-all(bf16[8,2,32768]{2,1,0:T(2,128)(2,1)S(1)} %reshape.55), channel_id=1, replica_groups=mesh['gx'=8,'gy'=2,'gz'=16] {'gx'}, dimensions={0} | all-to-all | bytes 2097152 | tf_op jit(solution)/shard_map/all_to_all | solution.py:17
  189.5 1.0 reshape.56
  190.5 0.3 copy.76
  190.8 0.6 copy.68
  191.4 21.6 %all_to_all.87 = bf16[8,128,512]{2,0,1:T(8,128)(2,1)S(1)} all-to-all(bf16[8,128,512]{2,0,1:T(8,128)(2,1)S(1)} %copy.68), channel_id=1, replica_groups=mesh['gx'=8,'gy'=2,'gz'=16] {'gz'}, dimensions={1} | all-to-all | bytes 2097152 | tf_op jit(solution)/shard_map/all_to_all | solution.py:17
  213.1 0.3 fusion.33
  213.4 0.4 multiply_reduce_fusion
  213.8 0.3 convert_bitcast_fusion
  214.4 0.4 copy-done.5
  214.8 0.3 fusion.17
  215.1 2.5 %fusion.23 = bf16[128,8,512]{2,0,1:T(8,128)(2,1)S(1)} fusion(f32[640,8,512]{2,0,1:T(8,128)} %copy-done.1, bf16[128,8,512]{2,1,0:T(8,128)(2,1)S(1)} %fusion.17, f32[8,512]{1,0:T(8,128)S(1)} %dynamic-slice_convert_fusion, bf16[128,128]{1,0:T(8,128)(2,1)S(1)} %copy-done), kind=kOutput, calls=%fused_computation.36 | convolution fusion | flops 137363456 | bytes 4243456 | tf_op jit(solution)/shard_map/hc,hij->cij/dot_general | solution.py:51
  217.7 0.6 copy.73
  218.3 19.6 %all_to_all.88 = bf16[128,8,512]{2,1,0:T(8,128)(2,1)S(1)} all-to-all(bf16[128,8,512]{2,1,0:T(8,128)(2,1)S(1)} %copy.73), channel_id=1, replica_groups=mesh['gx'=8,'gy'=2,'gz'=16] {'gz'}, dimensions={0} | all-to-all | bytes 2097152 | tf_op jit(solution)/shard_map/all_to_all | solution.py:17
  237.8 1.1 copy.92
  (32 shorter events, 1.8 us)
Async XLA Ops:
  6.5 208.6 %copy-start = (bf16[128,128]{1,0:T(8,128)(2,1)S(1)}, bf16[128,128]{1,0:T(8,128)(2,1)}, u32[]{:S(2)}) copy-start(bf16[128,128]{1,0:T(8,128)(2,1)} %param.13) | copy-start | bytes 98308
  6.5 10.3 %copy-start.2 = (bf16[4,128,128]{2,1,0:T(8,128)(2,1)S(1)}, bf16[4,128,128]{2,1,0:T(8,128)(2,1)}, u32[]{:S(2)}) copy-start(bf16[4,128,128]{2,1,0:T(8,128)(2,1)} %param.10) | copy-start | bytes 393220
  6.5 10.8 %copy-start.3 = (bf16[128,128]{1,0:T(8,128)(2,1)S(1)}, bf16[128,128]{1,0:T(8,128)(2,1)}, u32[]{:S(2)}) copy-start(bf16[128,128]{1,0:T(8,128)(2,1)} %param.11) | copy-start | bytes 98308
  9.4 22.0 %all-to-all-start = ((bf16[8,128,512]{2,0,1:T(8,128)(2,1)}), bf16[8,128,512]{2,0,1:T(8,128)(2,1)S(1)}, u32[]{:S(2)}, u32[]{:S(2)}) async-start(bf16[8,128,512]{2,0,1:T(8,128)(2,1)} %copy.62), calls=%async_computation | async-start | bytes 2097152 | tf_op jit(solution)/shard_map/all_to_all | solution.py:17
  16.7 15.1 %copy-start.4 = (f32[128]{0:T(128)S(1)}, f32[128]{0:T(128)}, u32[]{:S(2)}) copy-start(f32[128]{0:T(128)} %param.9) | copy-start | bytes 1540
  16.8 123.9 %all-gather.3.cloned.1.call-start = ((), (), s32[]{:S(2)}) async-start(), calls=%async_computation.6 | async-start | bytes 3145728 | tf_op jit(solution)/shard_map/all_gather | solution.py:43
  33.4 4.0 %copy-start.1 = (f32[640,8,512]{2,0,1:T(8,128)}, f32[640,8,512]{2,0,1:T(8,128)S(1)}, u32[]{:S(2)}) copy-start(f32[640,8,512]{2,0,1:T(8,128)S(1)} %fusion.30) | copy-start | bytes 31457284
  214.2 0.7 copy-start.5
Sparse Core Ops, SparseCore 0:
  130.2 10.4 all-gather.2

commit v2 on v1

v2 whole, which is shorter than its diff:
```python
import functools

import jax
import jax.numpy as jnp
from jax import lax
from jax.experimental import pallas as pl
from jax.experimental.pallas import tpu as pltpu
from jax.sharding import PartitionSpec as P

EPSILON = 1e-05
MESH = pl.DeviceIdType.MESH
PARTS = 2
LANES = 128


def statistics(values):
    average = jnp.mean(values, axis=0)
    centred = values - average
    return centred * lax.rsqrt(jnp.mean(jnp.square(centred), axis=0) + EPSILON)


def kernel(
    nx, ng,
    pair, mask, input_gain, input_weights, gate_weight, hidden_gain, out_weight,
    out,
    shared, sides, left_right, other_left, turned, triangle, hidden, update, gate,
    weights, gains, rows_in, rows_left, rows_right,
    send, got_shared, got_sides, got_left, got_hidden, got_out,
):
    x, y, g = lax.axis_index("gx"), lax.axis_index("gy"), lax.axis_index("gz")
    chips = nx * ng
    me = x * ng + g
    depth = pair.shape[0]
    rows = pair.shape[1] // ng
    width = pair.shape[2] // PARTS
    channels = gate_weight.shape[0]
    long = turned.shape[0]

    def device(chip):
        return (chip // ng, y, lax.rem(chip, ng))

    barrier = pltpu.get_barrier_semaphore()

    @pl.loop(1, chips)
    def _(step):
        pl.semaphore_signal(
            barrier, inc=1, device_id=device(lax.rem(me + step, chips)), device_id_type=MESH
        )

    pl.semaphore_signal(barrier, inc=1, device_id=(x, 1 - y, g), device_id_type=MESH)

    for k in range(4):
        weights[k * channels : (k + 1) * channels] = (
            input_weights[k].astype(jnp.float32).T.astype(jnp.bfloat16)
        )
    weights[4 * channels : 5 * channels] = gate_weight[...].astype(jnp.float32).T.astype(jnp.bfloat16)
    weights[5 * channels :] = out_weight[...].astype(jnp.float32).T.astype(jnp.bfloat16)
    gains[0] = jnp.broadcast_to(input_gain[...], (channels, channels)).T
    gains[1] = jnp.broadcast_to(hidden_gain[...], (channels, channels)).T

    pl.semaphore_wait(barrier, chips)

    my_rows = pl.ds(pl.multiple_of(g * rows, rows), rows)
    my_channels = pl.ds(pl.multiple_of(g * depth, depth), depth)
    for q in range(PARTS):
        columns = pl.ds(q * width, width)

        @pl.loop(1, ng)
        def _(step):
            peer = lax.rem(g + step, ng)
            pltpu.make_async_remote_copy(
                src_ref=pair.at[:, pl.ds(pl.multiple_of(peer * rows, rows), rows), columns],
                dst_ref=shared.at[q, my_channels],
                send_sem=send.at[0],
                recv_sem=got_shared.at[q],
                device_id=(x, y, peer),
                device_id_type=MESH,
            ).start()

        pltpu.make_async_copy(
            pair.at[:, my_rows, columns], shared.at[q, my_channels], got_shared.at[q]
        ).start()

    stride = rows
    block = pl.ds(pl.multiple_of(me * rows, rows), rows)
    for q in range(PARTS):
        pltpu.make_async_copy(shared.at[q], shared.at[q], got_shared.at[q]).wait()
        for at in range(width // LANES):
            lanes = pl.ds(at * LANES, LANES)
            normed = statistics(shared[q, :, :, lanes].astype(jnp.float32))
            rows_in[pl.ds(0, channels * rows)] = normed.reshape(channels * rows, LANES)
            share_mask = mask[my_rows, pl.ds(q * width + at * LANES, LANES)].astype(jnp.float32)
            rows_in[pl.ds(channels * rows, rows)] = share_mask

            @pl.loop(0, rows)
            def _(r):
                take = pl.ds(r, channels, stride=stride)
                one = (rows_in[take, :] * gains[0]).astype(jnp.bfloat16)
                product = jnp.dot(
                    weights[: 5 * channels], one, preferred_element_type=jnp.float32
                )
                keep = rows_in[pl.ds(channels * rows + r, 1), :]
                a, b, c, d, e = (product[k * channels : (k + 1) * channels] for k in range(5))
                rows_left[take, :] = keep * jax.nn.sigmoid(a) * b
                rows_right[take, :] = keep * jax.nn.sigmoid(c) * d
                gate[q * (width // LANES) + at, r] = keep * jax.nn.sigmoid(e)

            sides[q, :, 0, :, lanes] = (
                rows_left[...].reshape(channels, rows, LANES).astype(jnp.bfloat16)
            )
            sides[q, :, 1, :, lanes] = (
                rows_right[...].reshape(channels, rows, LANES).astype(jnp.bfloat16)
            )

        @pl.loop(1, chips)
        def _(step):
            owner = lax.rem(me + step, chips)
            pltpu.make_async_remote_copy(
                src_ref=sides.at[q, owner],
                dst_ref=left_right.at[q, :, block, :],
                send_sem=send.at[1],
                recv_sem=got_sides.at[q],
                device_id=device(owner),
                device_id_type=MESH,
            ).start()

        pltpu.make_async_copy(
            sides.at[q, me], left_right.at[q, :, block, :], got_sides.at[q]
        ).start()

    half = PARTS * width
    for q in range(PARTS):
        pltpu.make_async_copy(left_right.at[q], left_right.at[q], got_sides.at[q]).wait()
        pltpu.make_async_remote_copy(
            src_ref=left_right.at[q, 0],
            dst_ref=other_left.at[q],
            send_sem=send.at[2],
            recv_sem=got_left.at[q],
            device_id=(x, 1 - y, g),
            device_id_type=MESH,
        ).start()
        for at in range(width // LANES):
            turned[pl.ds(pl.multiple_of(y * half + q * width + at * LANES, LANES), LANES), :] = (
                left_right[q, 0, :, pl.ds(at * LANES, LANES)].T
            )
    for q in range(PARTS):
        pltpu.make_async_copy(other_left.at[q], other_left.at[q], got_left.at[q]).wait()
        for at in range(width // LANES):
            turned[
                pl.ds(pl.multiple_of((1 - y) * half + q * width + at * LANES, LANES), LANES), :
            ] = other_left[q, :, pl.ds(at * LANES, LANES)].T

    tall = rows * ng
    for q in range(PARTS):

        @pl.loop(0, nx)
        def _(step):
            plane = lax.rem(x + step, nx)
            some = pl.ds(pl.multiple_of(plane * tall, tall), tall)
            triangle[q, some, :] = jnp.dot(
                turned[some, :], left_right[q, 1], preferred_element_type=jnp.float32
            ).astype(jnp.bfloat16)

        @pl.loop(1, chips)
        def _(step):
            owner = lax.rem(me + step, chips)
            pltpu.make_async_remote_copy(
                src_ref=triangle.at[q, pl.ds(pl.multiple_of(owner * rows, rows), rows), :],
                dst_ref=hidden.at[q, me],
                send_sem=send.at[3],
                recv_sem=got_hidden.at[q],
                device_id=device(owner),
                device_id_type=MESH,
            ).start()

        pltpu.make_async_copy(
            triangle.at[q, block, :], hidden.at[q, me], got_hidden.at[q]
        ).start()

    for q in range(PARTS):
        columns = pl.ds(q * width, width)
        pltpu.make_async_copy(hidden.at[q], hidden.at[q], got_hidden.at[q]).wait()
        for at in range(width // LANES):
            lanes = pl.ds(at * LANES, LANES)
            normed = statistics(hidden[q, :, :, lanes].astype(jnp.float32))
            rows_in[pl.ds(0, channels * rows)] = normed.reshape(channels * rows, LANES)

            @pl.loop(0, rows)
            def _(r):
                take = pl.ds(r, channels, stride=stride)
                one = (rows_in[take, :] * gains[1]).astype(jnp.bfloat16)
                projected = jnp.dot(
                    weights[5 * channels :], one, preferred_element_type=jnp.float32
                )
                rows_left[take, :] = gate[q * (width // LANES) + at, r] * projected

            update[q, :, :, lanes] = (
                rows_left[...].reshape(channels, rows, LANES).astype(jnp.bfloat16)
            )

        @pl.loop(1, ng)
        def _(step):
            peer = lax.rem(g + step, ng)
            pltpu.make_async_remote_copy(
                src_ref=update.at[q, pl.ds(pl.multiple_of(peer * depth, depth), depth)],
                dst_ref=out.at[:, my_rows, columns],
                send_sem=send.at[4],
                recv_sem=got_out,
                device_id=(x, y, peer),
                device_id_type=MESH,
            ).start()

        pltpu.make_async_copy(update.at[q, my_channels], out.at[:, my_rows, columns], got_out).start()

    pltpu.make_async_copy(out, out, got_out).wait()
    for q in range(PARTS):
        few = shared.at[q, pl.ds(0, (ng - 1) * depth)]
        pltpu.make_async_copy(few, few, send.at[0]).wait()
        most = sides.at[q, pl.ds(0, chips - 1)]
        pltpu.make_async_copy(most, most, send.at[1]).wait()
        pltpu.make_async_copy(other_left.at[q], other_left.at[q], send.at[2]).wait()
        most = triangle.at[q, pl.ds(0, (chips - 1) * rows)]
        pltpu.make_async_copy(most, most, send.at[3]).wait()
        few = update.at[q, pl.ds(0, (ng - 1) * depth)]
        pltpu.make_async_copy(few, few, send.at[4]).wait()


def shards(mesh, pair, pair_mask, input_gain, input_weights, out_gate_weight, hidden_gain, out_weight):
    nx, ng = mesh.shape["gx"], mesh.shape["gz"]
    chips = nx * ng
    channels, hidden = input_weights.shape[1:]
    depth, tall, wide = pair.shape
    rows, width, long = tall // ng, wide // PARTS, tall * nx
    low, full = jnp.bfloat16, jnp.float32
    vmem = pl.BlockSpec(memory_space=pltpu.VMEM)
    return pl.pallas_call(
        functools.partial(kernel, nx, ng),
        out_shape=jax.ShapeDtypeStruct(pair.shape, low),
        in_specs=[vmem] * 7,
        out_specs=vmem,
        scratch_shapes=[
            pltpu.VMEM((PARTS, channels, rows, width), low),
            pltpu.VMEM((PARTS, hidden, 2, rows, width), low),
            pltpu.VMEM((PARTS, 2, long, width), low),
            pltpu.VMEM((PARTS, long, width), low),
            pltpu.VMEM((2 * wide, long), low),
            pltpu.VMEM((PARTS, long, width), low),
            pltpu.VMEM((PARTS, hidden, rows, width), low),
            pltpu.VMEM((PARTS, channels, rows, width), low),
            pltpu.VMEM((wide // LANES, rows, channels, LANES), full),
            pltpu.VMEM((6 * channels, channels), low),
            pltpu.VMEM((2, channels, channels), full),
            pltpu.VMEM((channels * rows + rows, LANES), full),
            pltpu.VMEM((channels * rows, LANES), full),
            pltpu.VMEM((channels * rows, LANES), full),
            pltpu.SemaphoreType.DMA((5,)),
            pltpu.SemaphoreType.DMA((PARTS,)),
            pltpu.SemaphoreType.DMA((PARTS,)),
            pltpu.SemaphoreType.DMA((PARTS,)),
            pltpu.SemaphoreType.DMA((PARTS,)),
            pltpu.SemaphoreType.DMA(()),
        ],
        compiler_params=pltpu.CompilerParams(collective_id=0, has_side_effects=True),
    )(
        pair, pair_mask, input_gain[None], input_weights, out_gate_weight, hidden_gain[None], out_weight
    )


def solution(mesh):
    placed = (P("gz", "gx", "gy"), P("gx", "gy"), P(), P(), P(), P(), P())
    return jax.shard_map(
        functools.partial(shards, mesh),
        mesh=mesh,
        in_specs=placed,
        out_specs=P("gz", "gx", "gy"),
        check_vma=False,
    )
```

time: 247 us -> 123 us (0.50)
  blocking collectives: 167 us -> 0 us
  Pallas kernels: 0 us -> 120 us
  waiting for transfers between devices: 23.7 us -> 0 us
  between operations: 13.7 us -> 0.01 us
  local copies, waits for them, and re-layouts: 15.8 us -> 2.26 us
  other arithmetic: 11.2 us -> 0 us
  starting transfers between devices: 7.43 us -> 0 us
  matrix products: 7.01 us -> 0 us
    all_to_all x5 -> x0, blocking collectives: 167 us -> none  [exchange(): lax.all_to_all(value, axis, split_axis=split_dim, concat_axis=concat_dim,...]
    pallas_call x0 -> x1, Pallas kernels: none -> 120 us  [shards(): pl.pallas_call(functools.partial(kernel, nx, ng), out_shape=jax.ShapeDtyp...]
    all_to_all x1 -> x0, waiting for transfers between devices: 13.1 us -> none  [exchange(): lax.all_to_all(value, axis, split_axis=split_dim, concat_axis=concat_dim,...]
    all_gather x1 -> x0, waiting for transfers between devices: 10.6 us -> none  [shards(): left_side = lax.all_gather(sides[:, 0], 'gy', axis=2, tiled=True)]
    all_to_all x1 -> x0, starting transfers between devices: 7.39 us -> none  [exchange(): lax.all_to_all(value, axis, split_axis=split_dim, concat_axis=concat_dim,...]
    unnamed x1 -> x0, other arithmetic: 7.04 us -> none
    dot_general x3 -> x0, matrix products: 7.01 us -> none  [the longest x1 2.87 us: shards(): jnp.einsum('hki,hkj->hij', left_side, sides[:, 1], preferred_element_type...]
    unnamed x26 -> x1, local copies, waits for them, and re-layouts: 9.09 us -> 2.26 us
  transfers between devices with their start and end apart: 2 -> 0, of which waited for: 2 -> 0; matrix products, arithmetic and copies ran while one was open for 1% -> 0% of each run, Pallas kernels for 0% -> 0%
where the time goes in v2:
time: 123 us; the launch traced here: 122 us
  Pallas kernels  120 us (98%)
  local copies, waits for them, and re-layouts  2.26 us (2%)
    pallas_call x1, Pallas kernels, shards(): pl.pallas_call(functools.partial(kernel, nx, ng), out_shape=jax.ShapeDtyp...  120 us

profile of v2, /device:TPU:8, one launch (start us, length us, event | category | flops | bytes accessed | tf_op | source)
XLA Modules:
  0.0 122.0 jit_solution(6866994066007033139)
XLA Ops:
  0.0 119.8 %shard_map.73 = bf16[8,128,512]{2,1,0:T(8,128)(2,1)} custom-call(bf16[8,128,512]{2,1,0:T(8,128)(2,1)} %pair.1, s32[128,512]{1,0:T(8,128)} %mask.1, f32[1,128]{1,0:T(1,128)} %bitcast.2, bf16[4,128,128]{2,1,0:T(8,128)(2,1)} %input_weights.1, bf16[128,128]{1,0:T(8,128)(2,1)} %gate_weight.1, f32[1,128]{1,0:T(1,128)} %bitcast.3, bf16[128,128]{1,0:T(8,128)(2,1)} %out_weight.1), custom_call_target="tpu_custom_call" | custom-call | tf_op jit(solution)/shard_map/pallas_call | solution.py:236
  119.8 2.3 %copy.9 = bf16[8,128,512]{2,1,0:T(8,128)(2,1)} copy(bf16[8,128,512]{2,1,0:T(8,128)(2,1)} %shard_map.73) | data formatting | bytes 2097152

commit v3 on v2

v3 whole, which is shorter than its diff:
```python
import functools

import jax
import jax.numpy as jnp
from jax import lax
from jax.experimental import pallas as pl
from jax.experimental.pallas import tpu as pltpu
from jax.sharding import PartitionSpec as P

EPSILON = 1e-05
MESH = pl.DeviceIdType.MESH
LANES = 128
PARTS = 4


def statistics(values):
    average = jnp.mean(values, axis=0)
    centred = values - average
    return centred * lax.rsqrt(jnp.mean(jnp.square(centred), axis=0) + EPSILON)


def kernel(
    nx, ng,
    pair_in, mask_in, input_gain, input_weights_in, gate_weight_in, hidden_gain, out_weight_in,
    out,
    pair, mask, input_weights, gate_weight, out_weight,
    shared, ones, left, right, all_left, all_right, other_left, turned, triangle, hidden, update, gate,
    weights, gains, rows_in, rows_out, rows_kept,
    loaded, send, got_shared, got_left, got_right, got_other, got_hidden, got_out, planes,
):
    x, y, g = lax.axis_index("gx"), lax.axis_index("gy"), lax.axis_index("gz")
    chips = nx * ng
    me = x * ng + g
    depth = pair.shape[0]
    rows = pair.shape[1] // ng
    channels = gate_weight.shape[0]
    wide = PARTS * LANES
    tall = ng * rows

    def plane_at(step):
        far = (step + 1) // 2
        return lax.rem(x + lax.rem(step, 2) * far + (1 - lax.rem(step, 2)) * (nx - far), nx)

    def aligned(at, size):
        return pl.ds(pl.multiple_of(at * size, size), size)

    barrier = pltpu.get_barrier_semaphore()

    @pl.loop(1, ng)
    def _(step):
        pl.semaphore_signal(
            barrier, inc=1, device_id=(x, y, lax.rem(g + step, ng)), device_id_type=MESH
        )

    @pl.loop(1, nx)
    def _(step):
        pl.semaphore_signal(barrier, inc=1, device_id=(plane_at(step), y, g), device_id_type=MESH)

    pl.semaphore_signal(barrier, inc=1, device_id=(x, 1 - y, g), device_id_type=MESH)

    loads = [
        pltpu.make_async_copy(there, here, loaded.at[k])
        for k, (there, here) in enumerate(
            (
                (pair_in, pair),
                (input_weights_in, input_weights),
                (gate_weight_in, gate_weight),
                (out_weight_in, out_weight),
                (mask_in, mask),
            )
        )
    ]
    for load in loads:
        load.start()
    gains[0] = jnp.broadcast_to(input_gain[...], (channels, channels)).T
    gains[1] = jnp.broadcast_to(hidden_gain[...], (channels, channels)).T
    for load in loads:
        load.wait()

    pl.semaphore_wait(barrier, ng + nx - 1)

    my_rows = aligned(g, rows)
    my_channels = aligned(g, depth)
    for q in range(PARTS):
        columns = pl.ds(q * LANES, LANES)

        @pl.loop(1, ng)
        def _(step):
            peer = lax.rem(g + step, ng)
            pltpu.make_async_remote_copy(
                src_ref=pair.at[:, aligned(peer, rows), columns],
                dst_ref=shared.at[q, my_channels],
                send_sem=send.at[0],
                recv_sem=got_shared.at[q],
                device_id=(x, y, peer),
                device_id_type=MESH,
            ).start()

        pltpu.make_async_copy(
            pair.at[:, my_rows, columns], shared.at[q, my_channels], got_shared.at[q]
        ).start()

    @pl.loop(1, nx)
    def _(step):
        pl.semaphore_signal(planes, inc=1, device_id=(plane_at(step), y, g), device_id_type=MESH)

    for k in range(4):
        weights[k * channels : (k + 1) * channels] = (
            input_weights[k].astype(jnp.float32).T.astype(jnp.bfloat16)
        )
    weights[4 * channels : 5 * channels] = gate_weight[...].astype(jnp.float32).T.astype(jnp.bfloat16)
    weights[5 * channels :] = out_weight[...].astype(jnp.float32).T.astype(jnp.bfloat16)

    block = aligned(me, rows)

    def to_owners(side, whole, got, q):
        @pl.loop(1, chips)
        def _(step):
            plane, column = plane_at(lax.rem(step, nx)), lax.rem(g + step // nx, ng)
            pltpu.make_async_remote_copy(
                src_ref=side.at[q, plane * ng + column],
                dst_ref=whole.at[q, block, :],
                send_sem=send.at[1],
                recv_sem=got.at[q],
                device_id=(plane, y, column),
                device_id_type=MESH,
            ).start()

        pltpu.make_async_copy(side.at[q, me], whole.at[q, block, :], got.at[q]).start()

    for q in range(PARTS):
        pltpu.make_async_copy(shared.at[q], shared.at[q], got_shared.at[q]).wait()
        normed = statistics(shared[q].astype(jnp.float32))
        rows_in[...] = normed.reshape(channels * rows, LANES)
        rows_kept[q] = mask[my_rows, pl.ds(q * LANES, LANES)].astype(jnp.float32)

        @pl.loop(0, rows)
        def _(r):
            take = pl.ds(r, channels, stride=rows)
            one = (rows_in[take, :] * gains[0]).astype(jnp.bfloat16)
            ones[q, r] = one
            product = jnp.dot(weights[: 2 * channels], one, preferred_element_type=jnp.float32)
            rows_out[take, :] = (
                rows_kept[q, pl.ds(r, 1), :]
                * jax.nn.sigmoid(product[:channels])
                * product[channels:]
            )

        left[q] = rows_out[...].reshape(channels, rows, LANES).astype(jnp.bfloat16)
        if q == 0:
            pl.semaphore_wait(planes, nx - 1)
        to_owners(left, all_left, got_left, q)

    for q in range(PARTS):

        @pl.loop(0, rows)
        def _(r):
            product = jnp.dot(
                weights[2 * channels : 5 * channels], ones[q, r], preferred_element_type=jnp.float32
            )
            keep = rows_kept[q, pl.ds(r, 1), :]
            rows_out[pl.ds(r, channels, stride=rows), :] = (
                keep * jax.nn.sigmoid(product[:channels]) * product[channels : 2 * channels]
            )
            gate[q, r] = keep * jax.nn.sigmoid(product[2 * channels :])

        right[q] = rows_out[...].reshape(channels, rows, LANES).astype(jnp.bfloat16)
        to_owners(right, all_right, got_right, q)

    for q in range(PARTS):
        pltpu.make_async_copy(all_left.at[q], all_left.at[q], got_left.at[q]).wait()
        pltpu.make_async_remote_copy(
            src_ref=all_left.at[q],
            dst_ref=other_left.at[q],
            send_sem=send.at[2],
            recv_sem=got_other.at[q],
            device_id=(x, 1 - y, g),
            device_id_type=MESH,
        ).start()
        turned[aligned(y * PARTS + q, LANES), :] = all_left[q].T
    for q in range(PARTS):
        pltpu.make_async_copy(other_left.at[q], other_left.at[q], got_other.at[q]).wait()
        turned[aligned((1 - y) * PARTS + q, LANES), :] = other_left[q].T

    for q in range(PARTS):
        pltpu.make_async_copy(all_right.at[q], all_right.at[q], got_right.at[q]).wait()

        @pl.loop(0, nx)
        def _(step):
            plane = plane_at(nx - 1 - step)
            some = aligned(plane, tall)
            triangle[q, some, :] = jnp.dot(
                turned[some, :], all_right[q], preferred_element_type=jnp.float32
            ).astype(jnp.bfloat16)

            @pl.loop(0, ng)
            def _(turn):
                column = lax.rem(g + turn, ng)

                @pl.when((step != nx - 1) | (turn != 0))
                def _():
                    pltpu.make_async_remote_copy(
                        src_ref=triangle.at[q, aligned(plane * ng + column, rows), :],
                        dst_ref=hidden.at[q, me],
                        send_sem=send.at[3],
                        recv_sem=got_hidden.at[q],
                        device_id=(plane, y, column),
                        device_id_type=MESH,
                    ).start()

        pltpu.make_async_copy(
            triangle.at[q, block, :], hidden.at[q, me], got_hidden.at[q]
        ).start()

    for q in range(PARTS):
        columns = pl.ds(q * LANES, LANES)
        pltpu.make_async_copy(hidden.at[q], hidden.at[q], got_hidden.at[q]).wait()
        normed = statistics(hidden[q].astype(jnp.float32))
        rows_in[...] = normed.reshape(channels * rows, LANES)

        @pl.loop(0, rows)
        def _(r):
            take = pl.ds(r, channels, stride=rows)
            one = (rows_in[take, :] * gains[1]).astype(jnp.bfloat16)
            projected = jnp.dot(weights[5 * channels :], one, preferred_element_type=jnp.float32)
            rows_out[take, :] = gate[q, r] * projected

        update[q] = rows_out[...].reshape(channels, rows, LANES).astype(jnp.bfloat16)

        @pl.loop(1, ng)
        def _(step):
            peer = lax.rem(g + step, ng)
            pltpu.make_async_remote_copy(
                src_ref=update.at[q, aligned(peer, depth)],
                dst_ref=out.at[:, my_rows, columns],
                send_sem=send.at[4],
                recv_sem=got_out,
                device_id=(x, y, peer),
                device_id_type=MESH,
            ).start()

        pltpu.make_async_copy(update.at[q, my_channels], out.at[:, my_rows, columns], got_out).start()

    pltpu.make_async_copy(out, out, got_out).wait()
    for q in range(PARTS):
        few = shared.at[q, pl.ds(0, (ng - 1) * depth)]
        pltpu.make_async_copy(few, few, send.at[0]).wait()
        for side in (left, right):
            most = side.at[q, pl.ds(0, chips - 1)]
            pltpu.make_async_copy(most, most, send.at[1]).wait()
        pltpu.make_async_copy(other_left.at[q], other_left.at[q], send.at[2]).wait()
        most = triangle.at[q, pl.ds(0, (chips - 1) * rows)]
        pltpu.make_async_copy(most, most, send.at[3]).wait()
        few = update.at[q, pl.ds(0, (ng - 1) * depth)]
        pltpu.make_async_copy(few, few, send.at[4]).wait()


def shards(mesh, pair, pair_mask, input_gain, input_weights, out_gate_weight, hidden_gain, out_weight):
    nx, ng = mesh.shape["gx"], mesh.shape["gz"]
    channels, hidden = input_weights.shape[1:]
    rows, long = pair.shape[1] // ng, pair.shape[1] * nx
    low, full = jnp.bfloat16, jnp.float32
    vmem, where = pl.BlockSpec(memory_space=pltpu.VMEM), pl.BlockSpec(memory_space=pl.ANY)
    parts = pltpu.SemaphoreType.DMA((PARTS,))
    return pl.pallas_call(
        functools.partial(kernel, nx, ng),
        out_shape=jax.ShapeDtypeStruct(pair.shape, low),
        in_specs=[where, where, vmem, where, where, vmem, where],
        out_specs=where,
        scratch_shapes=[
            pltpu.VMEM(pair.shape, low),
            pltpu.VMEM(pair_mask.shape, jnp.int32),
            pltpu.VMEM(input_weights.shape, low),
            pltpu.VMEM(out_gate_weight.shape, low),
            pltpu.VMEM(out_weight.shape, low),
            pltpu.VMEM((PARTS, channels, rows, LANES), low),
            pltpu.VMEM((PARTS, rows, channels, LANES), low),
            pltpu.VMEM((PARTS, hidden, rows, LANES), low),
            pltpu.VMEM((PARTS, hidden, rows, LANES), low),
            pltpu.VMEM((PARTS, long, LANES), low),
            pltpu.VMEM((PARTS, long, LANES), low),
            pltpu.VMEM((PARTS, long, LANES), low),
            pltpu.VMEM((2 * PARTS * LANES, long), low),
            pltpu.VMEM((PARTS, long, LANES), low),
            pltpu.VMEM((PARTS, hidden, rows, LANES), low),
            pltpu.VMEM((PARTS, channels, rows, LANES), low),
            pltpu.VMEM((PARTS, rows, channels, LANES), full),
            pltpu.VMEM((6 * channels, channels), low),
            pltpu.VMEM((2, channels, channels), full),
            pltpu.VMEM((channels * rows, LANES), full),
            pltpu.VMEM((channels * rows, LANES), full),
            pltpu.VMEM((PARTS, rows, LANES), full),
            pltpu.SemaphoreType.DMA((5,)),
            pltpu.SemaphoreType.DMA((5,)),
            parts,
            parts,
            parts,
            parts,
            parts,
            pltpu.SemaphoreType.DMA(()),
            pltpu.SemaphoreType.REGULAR,
        ],
        compiler_params=pltpu.CompilerParams(collective_id=0, has_side_effects=True),
    )(
        pair, pair_mask, input_gain[None], input_weights, out_gate_weight, hidden_gain[None], out_weight
    )


def solution(mesh):
    placed = (P("gz", "gx", "gy"), P("gx", "gy"), P(), P(), P(), P(), P())
    return jax.shard_map(
        functools.partial(shards, mesh),
        mesh=mesh,
        in_specs=placed,
        out_specs=P("gz", "gx", "gy"),
        check_vma=False,
    )
```

time: 123 us -> 98.7 us (0.80)
  Pallas kernels: 120 us -> 95.9 us
    pallas_call x1, Pallas kernels: 120 us -> 95.9 us  [shards(): pl.pallas_call(functools.partial(kernel, nx, ng), out_shape=jax.ShapeDtyp...]
where the time goes in v3:
time: 98.7 us; the launch traced here: 98.1 us
  Pallas kernels  95.9 us (97%)
  local copies, waits for them, and re-layouts  2.26 us (2%)
    pallas_call x1, Pallas kernels, shards(): pl.pallas_call(functools.partial(kernel, nx, ng), out_shape=jax.ShapeDtyp...  95.9 us
    unnamed x1, local copies, waits for them, and re-layouts  2.26 us

profile of v3, /device:TPU:8, one launch (start us, length us, event | category | flops | bytes accessed | tf_op | source)
XLA Modules:
  0.0 98.1 jit_solution(5585229807149834114)
XLA Ops:
  0.0 95.9 %shard_map.73 = bf16[8,128,512]{2,1,0:T(8,128)(2,1)} custom-call(bf16[8,128,512]{2,1,0:T(8,128)(2,1)} %pair_in.1, s32[128,512]{1,0:T(8,128)} %mask_in.1, f32[1,128]{1,0:T(1,128)} %bitcast.2, bf16[4,128,128]{2,1,0:T(8,128)(2,1)} %input_weights_in.1, bf16[128,128]{1,0:T(8,128)(2,1)} %gate_weight_in.1, f32[1,128]{1,0:T(1,128)} %bitcast.3, ...), custom_call_target="tpu_custom_call" | custom-call | tf_op jit(solution)/shard_map/pallas_call | solution.py:265
  95.9 2.3 %copy.9 = bf16[8,128,512]{2,1,0:T(8,128)(2,1)} copy(bf16[8,128,512]{2,1,0:T(8,128)(2,1)} %shard_map.73) | data formatting | bytes 2097152

commit v4 on v3

--- a/solution.py
+++ b/solution.py
@@ -134,7 +134,7 @@
         rows_in[...] = normed.reshape(channels * rows, LANES)
         rows_kept[q] = mask[my_rows, pl.ds(q * LANES, LANES)].astype(jnp.float32)
 
-        @pl.loop(0, rows)
+        @pl.loop(0, rows, unroll=8)
         def _(r):
             take = pl.ds(r, channels, stride=rows)
             one = (rows_in[take, :] * gains[0]).astype(jnp.bfloat16)
@@ -153,7 +153,7 @@
 
     for q in range(PARTS):
 
-        @pl.loop(0, rows)
+        @pl.loop(0, rows, unroll=8)
         def _(r):
             product = jnp.dot(
                 weights[2 * channels : 5 * channels], ones[q, r], preferred_element_type=jnp.float32
@@ -218,7 +218,7 @@
         normed = statistics(hidden[q].astype(jnp.float32))
         rows_in[...] = normed.reshape(channels * rows, LANES)
 
-        @pl.loop(0, rows)
+        @pl.loop(0, rows, unroll=8)
         def _(r):
             take = pl.ds(r, channels, stride=rows)
             one = (rows_in[take, :] * gains[1]).astype(jnp.bfloat16)
@@ -264,9 +264,9 @@
     parts = pltpu.SemaphoreType.DMA((PARTS,))
     return pl.pallas_call(
         functools.partial(kernel, nx, ng),
-        out_shape=jax.ShapeDtypeStruct(pair.shape, low),
+        out_shape=pltpu.VMEM(pair.shape, low),
         in_specs=[where, where, vmem, where, where, vmem, where],
-        out_specs=where,
+        out_specs=vmem,
         scratch_shapes=[
             pltpu.VMEM(pair.shape, low),
             pltpu.VMEM(pair_mask.shape, jnp.int32),

time: 98.7 us -> 95.2 us (0.965)
  Pallas kernels: 95.9 us -> 93.6 us
  local copies, waits for them, and re-layouts: 2.26 us -> 0.97 us
    pallas_call x1, Pallas kernels: 95.9 us -> 93.6 us  [shards(): pl.pallas_call(functools.partial(kernel, nx, ng), out_shape=pltpu.VMEM(pa...]
    unnamed x1, local copies, waits for them, and re-layouts: 2.26 us -> 0.97 us
where the time goes in v4:
time: 95.2 us; the launch traced here: 94.5 us
  Pallas kernels  93.6 us (98%)
  local copies, waits for them, and re-layouts  0.97 us (1%)
    pallas_call x1, Pallas kernels, shards(): pl.pallas_call(functools.partial(kernel, nx, ng), out_shape=pltpu.VMEM(pa...  93.6 us

profile of v4, /device:TPU:8, one launch (start us, length us, event | category | flops | bytes accessed | tf_op | source)
XLA Modules:
  0.0 94.5 jit_solution(16512026031562709700)
XLA Ops:
  0.0 93.6 %shard_map.73 = bf16[8,128,512]{2,1,0:T(8,128)(2,1)S(1)} custom-call(bf16[8,128,512]{2,1,0:T(8,128)(2,1)} %pair_in.1, s32[128,512]{1,0:T(8,128)} %mask_in.1, f32[1,128]{1,0:T(1,128)} %bitcast.2, bf16[4,128,128]{2,1,0:T(8,128)(2,1)} %input_weights_in.1, bf16[128,128]{1,0:T(8,128)(2,1)} %gate_weight_in.1, f32[1,128]{1,0:T(1,128)} %bitcast.3, ...), custom_call_target="tpu_custom_call" | custom-call | tf_op jit(solution)/shard_map/pallas_call | solution.py:265
  93.6 1.0 %copy.9 = bf16[8,128,512]{2,1,0:T(8,128)(2,1)} copy(bf16[8,128,512]{2,1,0:T(8,128)(2,1)S(1)} %shard_map.73) | data formatting | bytes 2097152

commit v5 on v4

--- a/solution.py
+++ b/solution.py
@@ -24,22 +24,28 @@
     pair_in, mask_in, input_gain, input_weights_in, gate_weight_in, hidden_gain, out_weight_in,
     out,
     pair, mask, input_weights, gate_weight, out_weight,
-    shared, ones, left, right, all_left, all_right, other_left, turned, triangle, hidden, update, gate,
+    shared, ones, left, right, all_left, all_right, other_left, turned, passed, partner, kept,
+    triangle, hidden, update, gate,
     weights, gains, rows_in, rows_out, rows_kept,
-    loaded, send, got_shared, got_left, got_right, got_other, got_hidden, got_out, planes,
+    loaded, send, got_shared, got_left, got_right, got_other, got_partner, got_hidden, got_out, planes,
 ):
     x, y, g = lax.axis_index("gx"), lax.axis_index("gy"), lax.axis_index("gz")
     chips = nx * ng
-    me = x * ng + g
+    reach = nx // 2
     depth = pair.shape[0]
     rows = pair.shape[1] // ng
     channels = gate_weight.shape[0]
     wide = PARTS * LANES
     tall = ng * rows
 
-    def plane_at(step):
-        far = (step + 1) // 2
-        return lax.rem(x + lax.rem(step, 2) * far + (1 - lax.rem(step, 2)) * (nx - far), nx)
+    def plane_at(far):
+        return lax.rem(x + far + nx, nx)
+
+    def owner_at(role, far):
+        plane = plane_at(far - role * 2 * far)
+        return plane, lax.rem(plane + nx - role, nx) * ng
+
+    owners = {(role, far): owner_at(role, far) for role in range(2) for far in range(reach)}
 
     def aligned(at, size):
         return pl.ds(pl.multiple_of(at * size, size), size)
@@ -52,9 +58,9 @@
             barrier, inc=1, device_id=(x, y, lax.rem(g + step, ng)), device_id_type=MESH
         )
 
-    @pl.loop(1, nx)
-    def _(step):
-        pl.semaphore_signal(barrier, inc=1, device_id=(plane_at(step), y, g), device_id_type=MESH)
+    line = [plane_at(far) for far in range(1 - reach, reach) if far]
+    for plane in line:
+        pl.semaphore_signal(barrier, inc=1, device_id=(plane, y, g), device_id_type=MESH)
 
     pl.semaphore_signal(barrier, inc=1, device_id=(x, 1 - y, g), device_id_type=MESH)
 
@@ -77,7 +83,7 @@
     for load in loads:
         load.wait()
 
-    pl.semaphore_wait(barrier, ng + nx - 1)
+    pl.semaphore_wait(barrier, ng + len(line))
 
     my_rows = aligned(g, rows)
     my_channels = aligned(g, depth)
@@ -100,9 +106,8 @@
             pair.at[:, my_rows, columns], shared.at[q, my_channels], got_shared.at[q]
         ).start()
 
-    @pl.loop(1, nx)
-    def _(step):
-        pl.semaphore_signal(planes, inc=1, device_id=(plane_at(step), y, g), device_id_type=MESH)
+    for plane in line:
+        pl.semaphore_signal(planes, inc=1, device_id=(plane, y, g), device_id_type=MESH)
 
     for k in range(4):
         weights[k * channels : (k + 1) * channels] = (
@@ -111,22 +116,34 @@
     weights[4 * channels : 5 * channels] = gate_weight[...].astype(jnp.float32).T.astype(jnp.bfloat16)
     weights[5 * channels :] = out_weight[...].astype(jnp.float32).T.astype(jnp.bfloat16)
 
-    block = aligned(me, rows)
-
     def to_owners(side, whole, got, q):
-        @pl.loop(1, chips)
-        def _(step):
-            plane, column = plane_at(lax.rem(step, nx)), lax.rem(g + step // nx, ng)
-            pltpu.make_async_remote_copy(
-                src_ref=side.at[q, plane * ng + column],
-                dst_ref=whole.at[q, block, :],
-                send_sem=send.at[1],
-                recv_sem=got.at[q],
-                device_id=(plane, y, column),
-                device_id_type=MESH,
-            ).start()
-
-        pltpu.make_async_copy(side.at[q, me], whole.at[q, block, :], got.at[q]).start()
+        def place(far):
+            return aligned(far * ng + g, rows)
+
+        def copies(turn, fars):
+            column = lax.rem(g + turn, ng)
+            for far in fars:
+                for role in range(2):
+                    plane, channel = owners[role, far]
+                    pltpu.make_async_remote_copy(
+                        src_ref=side.at[q, channel + column],
+                        dst_ref=whole.at[q, role, place(far), :],
+                        send_sem=send.at[1],
+                        recv_sem=got.at[q],
+                        device_id=(plane, y, column),
+                        device_id_type=MESH,
+                    ).start()
+
+        copies(0, range(reach - 1, 0, -1))
+
+        @pl.loop(1, ng)
+        def _(turn):
+            copies(turn, range(reach - 1, -1, -1))
+
+        for role in range(2):
+            pltpu.make_async_copy(
+                side.at[q, owners[role, 0][1] + g], whole.at[q, role, place(0), :], got.at[q]
+            ).start()
 
     for q in range(PARTS):
         pltpu.make_async_copy(shared.at[q], shared.at[q], got_shared.at[q]).wait()
@@ -148,7 +165,7 @@
 
         left[q] = rows_out[...].reshape(channels, rows, LANES).astype(jnp.bfloat16)
         if q == 0:
-            pl.semaphore_wait(planes, nx - 1)
+            pl.semaphore_wait(planes, len(line))
         to_owners(left, all_left, got_left, q)
 
     for q in range(PARTS):
@@ -177,40 +194,73 @@
             device_id=(x, 1 - y, g),
             device_id_type=MESH,
         ).start()
-        turned[aligned(y * PARTS + q, LANES), :] = all_left[q].T
+        for role in range(2):
+            turned[role, aligned(y * PARTS + q, LANES), :] = all_left[q, role].T
     for q in range(PARTS):
         pltpu.make_async_copy(other_left.at[q], other_left.at[q], got_other.at[q]).wait()
-        turned[aligned((1 - y) * PARTS + q, LANES), :] = other_left[q].T
+        for role in range(2):
+            turned[role, aligned((1 - y) * PARTS + q, LANES), :] = other_left[q, role].T
 
     for q in range(PARTS):
         pltpu.make_async_copy(all_right.at[q], all_right.at[q], got_right.at[q]).wait()
-
-        @pl.loop(0, nx)
-        def _(step):
-            plane = plane_at(nx - 1 - step)
-            some = aligned(plane, tall)
-            triangle[q, some, :] = jnp.dot(
-                turned[some, :], all_right[q], preferred_element_type=jnp.float32
-            ).astype(jnp.bfloat16)
-
-            @pl.loop(0, ng)
-            def _(turn):
+        for role in range(2):
+            side = 1 - 2 * role
+            other = plane_at(side)
+
+            def partial(plane):
+                return jnp.dot(
+                    turned[role, aligned(plane, tall), :],
+                    all_right[q, role],
+                    preferred_element_type=jnp.float32,
+                )
+
+            for far in range(reach):
+                passed[q, role, far] = partial(plane_at(side * (far + 1))).astype(jnp.bfloat16)
+            pltpu.make_async_remote_copy(
+                src_ref=passed.at[q, role],
+                dst_ref=partner.at[q, 1 - role],
+                send_sem=send.at[5],
+                recv_sem=got_partner.at[q],
+                device_id=(other, y, g),
+                device_id_type=MESH,
+            ).start()
+            for far in range(reach):
+                kept[q, role, far] = partial(plane_at(-side * far))
+
+    for q in range(PARTS):
+        pltpu.make_async_copy(partner.at[q], partner.at[q], got_partner.at[q]).wait()
+
+        for far in range(reach - 1, -1, -1):
+            for role in range(2):
+                triangle[q, role, far] = (
+                    kept[q, role, far] + partner[q, role, far].astype(jnp.float32)
+                ).astype(jnp.bfloat16)
+
+            def copies(turn):
                 column = lax.rem(g + turn, ng)
-
-                @pl.when((step != nx - 1) | (turn != 0))
-                def _():
+                for role in range(2):
                     pltpu.make_async_remote_copy(
-                        src_ref=triangle.at[q, aligned(plane * ng + column, rows), :],
-                        dst_ref=hidden.at[q, me],
+                        src_ref=triangle.at[q, role, far, aligned(column, rows), :],
+                        dst_ref=hidden.at[q, owners[role, 0][1] + g],
                         send_sem=send.at[3],
                         recv_sem=got_hidden.at[q],
-                        device_id=(plane, y, column),
+                        device_id=(owners[1 - role, far][0], y, column),
                         device_id_type=MESH,
                     ).start()
 
-        pltpu.make_async_copy(
-            triangle.at[q, block, :], hidden.at[q, me], got_hidden.at[q]
-        ).start()
+            if far:
+                copies(0)
+
+            @pl.loop(1, ng, unroll=5)
+            def _(turn):
+                copies(turn)
+
+        for role in range(2):
+            pltpu.make_async_copy(
+                triangle.at[q, role, 0, my_rows, :],
+                hidden.at[q, owners[role, 0][1] + g],
+                got_hidden.at[q],
+            ).start()
 
     for q in range(PARTS):
         columns = pl.ds(q * LANES, LANES)
@@ -246,10 +296,11 @@
         few = shared.at[q, pl.ds(0, (ng - 1) * depth)]
         pltpu.make_async_copy(few, few, send.at[0]).wait()
         for side in (left, right):
-            most = side.at[q, pl.ds(0, chips - 1)]
+            most = side.at[q, pl.ds(0, chips - 2)]
             pltpu.make_async_copy(most, most, send.at[1]).wait()
         pltpu.make_async_copy(other_left.at[q], other_left.at[q], send.at[2]).wait()
-        most = triangle.at[q, pl.ds(0, (chips - 1) * rows)]
+        pltpu.make_async_copy(passed.at[q], passed.at[q], send.at[5]).wait()
+        most = hidden.at[q, pl.ds(0, chips - 2)]
         pltpu.make_async_copy(most, most, send.at[3]).wait()
         few = update.at[q, pl.ds(0, (ng - 1) * depth)]
         pltpu.make_async_copy(few, few, send.at[4]).wait()
@@ -258,7 +309,8 @@
 def shards(mesh, pair, pair_mask, input_gain, input_weights, out_gate_weight, hidden_gain, out_weight):
     nx, ng = mesh.shape["gx"], mesh.shape["gz"]
     channels, hidden = input_weights.shape[1:]
-    rows, long = pair.shape[1] // ng, pair.shape[1] * nx
+    tall, reach = pair.shape[1], nx // 2
+    rows, near = tall // ng, tall * reach
     low, full = jnp.bfloat16, jnp.float32
     vmem, where = pl.BlockSpec(memory_space=pltpu.VMEM), pl.BlockSpec(memory_space=pl.ANY)
     parts = pltpu.SemaphoreType.DMA((PARTS,))
@@ -277,11 +329,14 @@
             pltpu.VMEM((PARTS, rows, channels, LANES), low),
             pltpu.VMEM((PARTS, hidden, rows, LANES), low),
             pltpu.VMEM((PARTS, hidden, rows, LANES), low),
-            pltpu.VMEM((PARTS, long, LANES), low),
-            pltpu.VMEM((PARTS, long, LANES), low),
-            pltpu.VMEM((PARTS, long, LANES), low),
-            pltpu.VMEM((2 * PARTS * LANES, long), low),
-            pltpu.VMEM((PARTS, long, LANES), low),
+            pltpu.VMEM((PARTS, 2, near, LANES), low),
+            pltpu.VMEM((PARTS, 2, near, LANES), low),
+            pltpu.VMEM((PARTS, 2, near, LANES), low),
+            pltpu.VMEM((2, 2 * PARTS * LANES, near), low),
+            pltpu.VMEM((PARTS, 2, reach, tall, LANES), low),
+            pltpu.VMEM((PARTS, 2, reach, tall, LANES), low),
+            pltpu.VMEM((PARTS, 2, reach, tall, LANES), full),
+            pltpu.VMEM((PARTS, 2, reach, tall, LANES), low),
             pltpu.VMEM((PARTS, hidden, rows, LANES), low),
             pltpu.VMEM((PARTS, channels, rows, LANES), low),
             pltpu.VMEM((PARTS, rows, channels, LANES), full),
@@ -291,7 +346,8 @@
             pltpu.VMEM((channels * rows, LANES), full),
             pltpu.VMEM((PARTS, rows, LANES), full),
             pltpu.SemaphoreType.DMA((5,)),
-            pltpu.SemaphoreType.DMA((5,)),
+            pltpu.SemaphoreType.DMA((6,)),
+            parts,
             parts,
             parts,
             parts,

time: 95.2 us -> 92.5 us (0.972)
  Pallas kernels: 93.6 us -> 91.4 us
    pallas_call x1, Pallas kernels: 93.6 us -> 91.4 us  [shards(): pl.pallas_call(functools.partial(kernel, nx, ng), out_shape=pltpu.VMEM(pa...]
where the time goes in v5:
time: 92.5 us; the launch traced here: 92.3 us
  Pallas kernels  91.4 us (99%)
  local copies, waits for them, and re-layouts  0.97 us (1%)
    pallas_call x1, Pallas kernels, shards(): pl.pallas_call(functools.partial(kernel, nx, ng), out_shape=pltpu.VMEM(pa...  91.4 us

profile of v5, /device:TPU:8, one launch (start us, length us, event | category | flops | bytes accessed | tf_op | source)
XLA Modules:
  0.0 92.3 jit_solution(969240267538581757)
XLA Ops:
  0.0 91.4 %shard_map.73 = bf16[8,128,512]{2,1,0:T(8,128)(2,1)S(1)} custom-call(bf16[8,128,512]{2,1,0:T(8,128)(2,1)} %pair_in.1, s32[128,512]{1,0:T(8,128)} %mask_in.1, f32[1,128]{1,0:T(1,128)} %bitcast.2, bf16[4,128,128]{2,1,0:T(8,128)(2,1)} %input_weights_in.1, bf16[128,128]{1,0:T(8,128)(2,1)} %gate_weight_in.1, f32[1,128]{1,0:T(1,128)} %bitcast.3, ...), custom_call_target="tpu_custom_call" | custom-call | tf_op jit(solution)/shard_map/pallas_call | solution.py:317
  91.4 1.0 %copy.9 = bf16[8,128,512]{2,1,0:T(8,128)(2,1)} copy(bf16[8,128,512]{2,1,0:T(8,128)(2,1)S(1)} %shard_map.73) | data formatting | bytes 2097152

commit v6 on v5

--- a/solution.py
+++ b/solution.py
@@ -50,13 +50,24 @@
     def aligned(at, size):
         return pl.ds(pl.multiple_of(at * size, size), size)
 
+    def far_first():
+        side = round(ng**0.5)
+        apart = [(dy, dx) for dy in range(side) for dx in range(side) if dy or dx]
+
+        def hops(d):
+            return min(d, side - d)
+
+        apart.sort(key=lambda d: -(hops(d[0]) + hops(d[1])))
+        return [
+            lax.rem(g // side + dy, side) * side + lax.rem(lax.rem(g, side) + dx, side)
+            for dy, dx in apart
+        ]
+
+    peers = far_first()
     barrier = pltpu.get_barrier_semaphore()
 
-    @pl.loop(1, ng)
-    def _(step):
-        pl.semaphore_signal(
-            barrier, inc=1, device_id=(x, y, lax.rem(g + step, ng)), device_id_type=MESH
-        )
+    for peer in peers:
+        pl.semaphore_signal(barrier, inc=1, device_id=(x, y, peer), device_id_type=MESH)
 
     line = [plane_at(far) for far in range(1 - reach, reach) if far]
     for plane in line:
@@ -90,9 +101,7 @@
     for q in range(PARTS):
         columns = pl.ds(q * LANES, LANES)
 
-        @pl.loop(1, ng)
-        def _(step):
-            peer = lax.rem(g + step, ng)
+        for peer in peers:
             pltpu.make_async_remote_copy(
                 src_ref=pair.at[:, aligned(peer, rows), columns],
                 dst_ref=shared.at[q, my_channels],
@@ -201,7 +210,7 @@
         for role in range(2):
             turned[role, aligned((1 - y) * PARTS + q, LANES), :] = other_left[q, role].T
 
-    for q in range(PARTS):
+    def swap(q):
         pltpu.make_async_copy(all_right.at[q], all_right.at[q], got_right.at[q]).wait()
         for role in range(2):
             side = 1 - 2 * role
@@ -227,7 +236,7 @@
             for far in range(reach):
                 kept[q, role, far] = partial(plane_at(-side * far))
 
-    for q in range(PARTS):
+    def finish(q):
         pltpu.make_async_copy(partner.at[q], partner.at[q], got_partner.at[q]).wait()
 
         for far in range(reach - 1, -1, -1):
@@ -263,6 +272,13 @@
             ).start()
 
     for q in range(PARTS):
+        swap(q)
+        if q > 1:
+            finish(q - 2)
+    for q in range(PARTS - 2, PARTS):
+        finish(q)
+
+    for q in range(PARTS):
         columns = pl.ds(q * LANES, LANES)
         pltpu.make_async_copy(hidden.at[q], hidden.at[q], got_hidden.at[q]).wait()
         normed = statistics(hidden[q].astype(jnp.float32))
@@ -277,9 +293,7 @@
 
         update[q] = rows_out[...].reshape(channels, rows, LANES).astype(jnp.bfloat16)
 
-        @pl.loop(1, ng)
-        def _(step):
-            peer = lax.rem(g + step, ng)
+        for peer in peers:
             pltpu.make_async_remote_copy(
                 src_ref=update.at[q, aligned(peer, depth)],
                 dst_ref=out.at[:, my_rows, columns],

time: 92.5 us -> 91.2 us (0.986)
  Pallas kernels: 91.4 us -> 90.1 us
    pallas_call x1, Pallas kernels: 91.4 us -> 90.1 us  [shards(): pl.pallas_call(functools.partial(kernel, nx, ng), out_shape=pltpu.VMEM(pa...]
where the time goes in v6:
time: 91.2 us; the launch traced here: 91.1 us
  Pallas kernels  90.1 us (99%)
  local copies, waits for them, and re-layouts  0.97 us (1%)
    pallas_call x1, Pallas kernels, shards(): pl.pallas_call(functools.partial(kernel, nx, ng), out_shape=pltpu.VMEM(pa...  90.1 us

profile of v6, /device:TPU:8, one launch (start us, length us, event | category | flops | bytes accessed | tf_op | source)
XLA Modules:
  0.0 91.1 jit_solution(7603063471069094380)
XLA Ops:
  0.0 90.1 %shard_map.73 = bf16[8,128,512]{2,1,0:T(8,128)(2,1)S(1)} custom-call(bf16[8,128,512]{2,1,0:T(8,128)(2,1)} %pair_in.1, s32[128,512]{1,0:T(8,128)} %mask_in.1, f32[1,128]{1,0:T(1,128)} %bitcast.2, bf16[4,128,128]{2,1,0:T(8,128)(2,1)} %input_weights_in.1, bf16[128,128]{1,0:T(8,128)(2,1)} %gate_weight_in.1, f32[1,128]{1,0:T(1,128)} %bitcast.3, ...), custom_call_target="tpu_custom_call" | custom-call | tf_op jit(solution)/shard_map/pallas_call | solution.py:331
  90.1 1.0 %copy.9 = bf16[8,128,512]{2,1,0:T(8,128)(2,1)} copy(bf16[8,128,512]{2,1,0:T(8,128)(2,1)S(1)} %shard_map.73) | data formatting | bytes 2097152

commit v7 on v6

--- a/solution.py
+++ b/solution.py
@@ -143,11 +143,11 @@
                         device_id_type=MESH,
                     ).start()
 
-        copies(0, range(reach - 1, 0, -1))
+        copies(0, range(1, reach))
 
         @pl.loop(1, ng)
         def _(turn):
-            copies(turn, range(reach - 1, -1, -1))
+            copies(turn, range(reach))
 
         for role in range(2):
             pltpu.make_async_copy(

time: 91.2 us -> 91.2 us (level)
  no operation moved by 1% of the time
where the time goes in v7:
time: 91.2 us; the launch traced here: 91.1 us
  Pallas kernels  90.1 us (99%)
  local copies, waits for them, and re-layouts  0.97 us (1%)
    pallas_call x1, Pallas kernels, shards(): pl.pallas_call(functools.partial(kernel, nx, ng), out_shape=pltpu.VMEM(pa...  90.1 us

profile of v7, /device:TPU:8, one launch (start us, length us, event | category | flops | bytes accessed | tf_op | source)
XLA Modules:
  0.0 91.1 jit_solution(14876366696782653320)
XLA Ops:
  0.0 90.1 %shard_map.73 = bf16[8,128,512]{2,1,0:T(8,128)(2,1)S(1)} custom-call(bf16[8,128,512]{2,1,0:T(8,128)(2,1)} %pair_in.1, s32[128,512]{1,0:T(8,128)} %mask_in.1, f32[1,128]{1,0:T(1,128)} %bitcast.2, bf16[4,128,128]{2,1,0:T(8,128)(2,1)} %input_weights_in.1, bf16[128,128]{1,0:T(8,128)(2,1)} %gate_weight_in.1, f32[1,128]{1,0:T(1,128)} %bitcast.3, ...), custom_call_target="tpu_custom_call" | custom-call | tf_op jit(solution)/shard_map/pallas_call | solution.py:331
  90.1 1.0 %copy.9 = bf16[8,128,512]{2,1,0:T(8,128)(2,1)} copy(bf16[8,128,512]{2,1,0:T(8,128)(2,1)S(1)} %shard_map.73) | data formatting | bytes 2097152
